TPU v7x, 32 devices: a whole 2x2x4 slice. The times are simulated.
32 devices in a mesh: gx: 4 (over y, core), gy: 4 (over z), gz: 2 (over x).
Axes of the slice: x: 2, y: 2, z: 4, core: 2. Of those that a mesh axis runs over, the one named last changes fastest.
Arguments:
- positions: float32 [3, 4, 8, 16, 128], P(None, 'gx', 'gy', 'gz'), may hold values from 0 to 1
- velocities: float32 [3, 4, 8, 16, 128], P(None, 'gx', 'gy', 'gz'), may hold values from -6 to 6
- occupancy: int32 [4, 8, 16], P('gx', 'gy', 'gz'), may hold values from 0 to 128, as said below
- mover_pos: float32 [3, 12, 4, 2, 128], P(None, 'gx', 'gy', 'gz'), may hold values from 0 to 1
- mover_vel: float32 [3, 12, 4, 2, 128], P(None, 'gx', 'gy', 'gz'), may hold values from -6 to 6
- mover_count: int32 [12, 4, 2], P('gx', 'gy', 'gz'), may hold values from 1 to 128
- mover_owner: int32 [12, 4, 2], P('gx', 'gy', 'gz'), may hold values from 0 to 3, as said below
- mover_cell: int32 [12, 4, 2], P('gx', 'gy', 'gz'), may hold values from 0 to 15, as said below
Outputs:
- new_positions: float32 [3, 4, 8, 16, 128], P(None, 'gx', 'gy', 'gz')
- new_velocities: float32 [3, 4, 8, 16, 128], P(None, 'gx', 'gy', 'gz')
Inputs may be any that keep to these rules, and one draw needn't show every extreme that they name: `mover_owner`: all leaving blocks of one device go to one owner in the device's own line along gx; at most 6 blocks arrive at one device, and in every draw some device takes 2 * 3 and some takes none. `mover_cell`: the cells named by the blocks that arrive at one device are distinct, and their occupancy is 0. Exactly 6 cells of each device have occupancy 0; every other cell holds 32 or more particles, and one cell of each device holds 128.
All inputs are finite; a program needn't handle non-finite values.
Results may differ from a plain program's by a relative error of at most 0.0001.
Values sent between devices are 32-bit elements; how exact they have to be, the bound alone decides.
A program may use at most 64 MiB of HBM per device.

v0:
```python
import functools

import jax
import jax.numpy as jnp
from jax import lax
from jax.experimental import pallas as pl
from jax.experimental.pallas import tpu as pltpu
from jax.sharding import PartitionSpec as P

eps_soft = 0.05
kick_step = 0.02
drift_step = 0.1
far_away = 1000.0

f32, bf16 = jnp.float32, jnp.bfloat16


def offsets(count):
    return sorted({0, 1 % count, count - 1})


def halo_steps():
    steps = [
        (dx, dy, dz)
        for dx in (-1, 0, 1)
        for dy in (-1, 0, 1)
        for dz in (-1, 0, 1)
        if (dx, dy, dz) != (0, 0, 0)
    ]
    return sorted(steps, key=lambda step: -sum(abs(d) for d in step))


def row_index(shape):
    return lax.broadcasted_iota(jnp.int32, shape, len(shape) - 2)


def exchange_kernel(
    axes, dims, leaving, occ_s, count_s, owner_s, cell_s, pos_ref, vel_ref, mpos_ref, mvel_ref,
    halo_ref, velm_ref, line, mov, send, recv, msend, mrecv
):
    nx, ny, nz = axes
    sx, sy, sz = dims
    slots = pos_ref.shape[-1]
    me = [lax.axis_index(name) for name in ("gx", "gy", "gz")]

    def device(step):
        return tuple(lax.rem(m + s, n) for m, s, n in zip(me, step, axes))

    near = sorted(
        {tuple(d % n for d, n in zip(step, axes)) for step in halo_steps()} - {(0, 0, 0)}
    )
    far = [ox for ox in range(nx) if ox not in offsets(nx)]

    def along_line(body, start):
        if nx <= 4:
            for ox in range(start, nx):
                body(ox)
        else:
            lax.fori_loop(start, nx, lambda ox, carry: (body(ox), carry)[1], 0)

    def halo_copy(step):
        source, target = [], []
        for d, size in zip(step, dims):
            if d == 0:
                source.append(pl.ds(1, size))
                target.append(pl.ds(1, size))
            elif d == 1:
                source.append(pl.ds(size, 1))
                target.append(pl.ds(0, 1))
            else:
                source.append(pl.ds(1, 1))
                target.append(pl.ds(size + 1, 1))
        number = (step[0] + 1) * 9 + (step[1] + 1) * 3 + step[2] + 1
        return pltpu.make_async_remote_copy(
            src_ref=halo_ref.at[(*source, pl.ds(0, 3))],
            dst_ref=halo_ref.at[(*target, pl.ds(0, 3))],
            send_sem=send.at[number],
            recv_sem=recv.at[number],
            device_id=device([d % n for d, n in zip(step, axes)]),
            device_id_type=pl.DeviceIdType.MESH,
        )

    def mover_copy(ox):
        return pltpu.make_async_remote_copy(
            src_ref=mov,
            dst_ref=line.at[pl.ds(me[0] * leaving, leaving)],
            send_sem=msend.at[ox],
            recv_sem=mrecv.at[ox],
            device_id=device((ox, 0, 0)),
            device_id_type=pl.DeviceIdType.MESH,
        )

    barrier = pltpu.get_barrier_semaphore()

    def greet(step):
        pl.semaphore_signal(
            barrier, inc=1, device_id=device(step), device_id_type=pl.DeviceIdType.MESH
        )

    for step in near:
        greet(step)
    if nx <= 4:
        for ox in far:
            greet((ox, 0, 0))
    else:
        lax.fori_loop(2, nx - 1, lambda ox, carry: (greet((ox, 0, 0)), carry)[1], 0)

    lane = lax.broadcasted_iota(jnp.int32, (1, slots), 1)
    base = me[0] * (sx * sy * sz)
    for b in range(leaving):
        live = lane < count_s[b]
        rows = [jnp.where(live, mpos_ref[k, b], far_away) for k in range(3)]
        rows += [mvel_ref[k, b] for k in range(3)]
        label = owner_s[b] * (sx * sy * sz) + cell_s[b]
        rows += [jnp.full((1, slots), label, jnp.int32).astype(f32)] * 2
        for k, row in enumerate(rows):
            mov[b, k : k + 1, :] = row
            line[me[0] * leaving + b, k : k + 1, :] = row

    pl.semaphore_wait(barrier, len(near) + len(far))
    along_line(lambda ox: mover_copy(ox).start(), 1)

    sub = row_index((sz, slots))
    lanes = lax.broadcasted_iota(jnp.int32, (sz, slots), 1)
    planes, where = [], []
    for x in range(sx):
        for y in range(sy):
            counts = jnp.zeros((sz, slots), jnp.int32)
            for z in range(sz):
                counts = jnp.where(sub == z, occ_s[x, y, z], counts)
            live = lanes < counts
            planes.append(
                [jnp.where(live, pos_ref[k, x, y], far_away) for k in range(3)]
                + [vel_ref[k, x, y] for k in range(3)]
            )
            where.append((sub + (base + (x * sy + y) * sz)).astype(f32))
    along_line(lambda ox: mover_copy(ox).wait(), 1)

    def merge(b, planes):
        rows = [line[b, pl.ds(k, 1), :] for k in range(7)]
        out = []
        for plane, here in zip(planes, where):
            hit = here == rows[6]
            out.append([jnp.where(hit, row, old) for row, old in zip(rows, plane)])
        return out

    if nx <= 4:
        for b in range(nx * leaving):
            planes = merge(b, planes)
    else:
        planes = lax.fori_loop(0, nx * leaving, merge, planes)

    flat = halo_ref.reshape((sx + 2) * (sy + 2) * (sz + 2) * 8, slots)
    for x in range(sx):
        for y in range(sy):
            first = (((x + 1) * (sy + 2) + y + 1) * (sz + 2) + 1) * 8
            for k in range(3):
                flat[pl.ds(first + k, sz, stride=8), :] = planes[x * sy + y][k]
    for step in halo_steps():
        halo_copy(step).start()
    for x in range(sx):
        for y in range(sy):
            for k in range(3):
                velm_ref[k, x, y] = planes[x * sy + y][3 + k]
    for step in halo_steps():
        halo_copy(step).wait()


def split(value):
    high = value.astype(bf16).astype(f32)
    rest = value - high
    middle = rest.astype(bf16).astype(f32)
    return high, middle, rest - middle


def stack(high, middle, low):
    return jnp.concatenate([high, high, high, middle, middle, low], -2).astype(bf16)


def force_kernel(
    dims, unroll, halo_ref, vel_ref, npos_ref, nvel_ref, left, left2, right, right2, src, src2, total
):
    sx, sy, sz = dims
    hx, hy, hz = (size + 2 for size in dims)
    slots = halo_ref.shape[-1]
    sub = row_index((8, slots))

    def centre(x, y):
        return x - 1 - 0.5 * sx, y - 1 - 0.5 * sy

    def sources(x, y):
        ox, oy = centre(x, y)
        shift = jnp.where(sub == 0, ox, jnp.where(sub == 1, oy, -0.5)).astype(f32)
        out = []
        for z in range(hz):
            extra = jnp.where(sub == 6, 1.0, jnp.where(sub == 7, float(z - 1 - sz // 2), 0.0))
            at = jnp.where(sub < 3, halo_ref[x, y, z] + shift, 0.0)
            high, middle, low = split(at + pltpu.roll(at * at, 3, 0) + extra.astype(f32))
            both = jnp.concatenate([high, middle], 0).astype(bf16)
            out.append((stack(high, middle, low), jnp.concatenate([both, both], 1)))
        return out

    def prepare(x):
        for y in range(1, sy + 1):
            for z, (keys, twice) in enumerate(sources(x, y)):
                left[x, y - 1, z] = keys.T
                src[x, y - 1, z] = twice
        for pair in range(sy // 2):
            low, up = sources(x, 2 * pair), sources(x, 2 * pair + 3)
            for z in range(hz):
                left2[x, pair, z] = jnp.concatenate([low[z][0], up[z][0]], 0).T
                src2[x, pair, z] = jnp.concatenate([low[z][1], up[z][1]], 0)

    def targets(x, pair, z):
        tiles = []
        for y in (2 * pair, 2 * pair + 1):
            ox, oy = centre(x + 1, y + 1)
            shift = jnp.where(sub == 0, ox, jnp.where(sub == 1, oy, -0.5)).astype(f32)
            at = halo_ref[x + 1, y + 1, z + 1]
            tiles.append(jnp.where(at < 0.5 * far_away, at, 0.5) + shift)
        zero = jnp.zeros((48, slots), bf16)
        for e in (-1, 0, 1):
            keys = []
            for at in tiles:
                at = jnp.where(sub < 3, at - jnp.where(sub == 2, float(e), 0.0).astype(f32), 0.0)
                norm = jnp.sum(at * at, axis=0, keepdims=True) + eps_soft
                key = jnp.where(sub < 3, -2.0 * at, jnp.where(sub < 6, 1.0, norm))
                key = jnp.where(sub < 7, key, 0.0)
                high, middle, low = split(key)
                keys.append(
                    jnp.concatenate([high, middle, low, high, middle, high], 0).astype(bf16)
                )
            right[x, pair, z, e + 1] = jnp.concatenate(keys, 1)
            right2[x, pair, z, e + 1] = jnp.concatenate(
                [jnp.concatenate([keys[0], zero], 1), jnp.concatenate([zero, keys[1]], 1)], 0
            )

    def weights(t):
        y = lax.rsqrt(t)
        a = jnp.maximum((1.0 + eps_soft) - t, 0.0) * y
        w = a * a * y
        high = w.astype(bf16)
        return jnp.concatenate([high, (w - high.astype(f32)).astype(bf16)], 0)

    def accumulate(steps, sums):
        lag = 2

        def distances(n):
            return jnp.dot(steps[n][0][...], steps[n][1][...], preferred_element_type=f32)

        queue, ready = [distances(0)], []
        for n in range(len(steps) + lag):
            if n < len(steps):
                if n + 1 < len(steps):
                    queue.append(distances(n + 1))
                ready.append(weights(queue.pop(0)))
            if n >= lag:
                step = steps[n - lag]
                sums[step[3]] = sums[step[3]] + jnp.dot(
                    step[2][...], ready.pop(0), preferred_element_type=f32
                )
        return sums

    def steps_of(x, pair, z, slot):
        steps = []
        for e in range(3):
            for dx in range(3):
                for y in (2 * pair, 2 * pair + 1):
                    steps.append((
                        left.at[x + dx, y, z + e], right.at[x, pair, z, e],
                        src.at[x + dx, y, z + e], 2 * slot,
                    ))
        for e in range(3):
            for dx in range(3):
                steps.append((
                    left2.at[x + dx, pair, z + e], right2.at[x, pair, z, e],
                    src2.at[x + dx, pair, z + e], 2 * slot + 1,
                ))
        return steps

    for x in range(hx):
        prepare(x)
    for x in range(sx):
        for pair in range(sy // 2):
            for z in range(sz):
                targets(x, pair, z)
    for x in range(sx):
        for pair in range(sy // 2):

            def body(i, carry, x=x, pair=pair):
                steps, sums = [], []
                for u in range(unroll):
                    steps += steps_of(x, pair, i * unroll + u, u)
                    sums += [jnp.zeros((16, 2 * slots), f32), jnp.zeros((32, 2 * slots), f32)]
                sums = accumulate(steps, sums)
                for u in range(unroll):
                    one, two = sums[2 * u], sums[2 * u + 1]
                    z = i * unroll + u
                    total[x, pair, 0, z] = one[:, :slots] + two[:16, :slots]
                    total[x, pair, 1, z] = one[:, slots:] + two[16:, slots:]
                return carry

            lax.fori_loop(0, sz // unroll, body, 0)

    flat = halo_ref.reshape(hx * hy * hz * 8, slots)
    for x in range(sx):
        for y in range(sy):
            sums = total.at[x, y // 2, y % 2].reshape(sz * 16, slots)

            def row(r, sums=sums):
                return sums[pl.ds(r, sz, stride=16), :]

            first = (((x + 1) * hy + y + 1) * hz + 1) * 8
            ox, oy = centre(x + 1, y + 1)
            zat = (row_index((sz, slots)) - sz // 2).astype(f32)
            live = None
            for k, shift in enumerate((ox, oy, -0.5)):
                raw = flat[pl.ds(first + k, sz, stride=8), :]
                if k == 0:
                    live = raw < 0.5 * far_away
                high, middle, low = split(raw + shift)
                at, sum_s = high + middle, row(k) + row(8 + k)
                if k == 2:
                    at, sum_s = at + zat, sum_s + row(7)
                force = sum_s - at * row(6)
                vel = jnp.where(live, vel_ref[k, x, y] + kick_step * force, 0.0)
                nvel_ref[k, x, y] = vel
                npos_ref[k, x, y] = jnp.where(live, raw + drift_step * vel, 0.0)


def exchange(occupancy, count, owner, cell, pos, vel, mpos, mvel):
    axes = tuple(lax.axis_size(name) for name in ("gx", "gy", "gz"))
    dims, leaving, slots = pos.shape[1:4], mpos.shape[1], mpos.shape[3]
    padded = tuple(size + 2 for size in dims) + (8, slots)
    vmem = pl.BlockSpec(memory_space=pltpu.VMEM)
    return pl.pallas_call(
        functools.partial(exchange_kernel, axes, dims, leaving),
        out_shape=(pltpu.VMEM(padded, f32), pltpu.VMEM(vel.shape, f32)),
        in_specs=[pl.BlockSpec(memory_space=pltpu.SMEM)] * 4 + [vmem] * 4,
        out_specs=(vmem, vmem),
        scratch_shapes=[
            pltpu.VMEM((axes[0] * leaving, 8, slots), f32),
            pltpu.VMEM((leaving, 8, slots), f32),
            pltpu.SemaphoreType.DMA((27,)),
            pltpu.SemaphoreType.DMA((27,)),
            pltpu.SemaphoreType.DMA((axes[0],)),
            pltpu.SemaphoreType.DMA((axes[0],)),
        ],
        compiler_params=pltpu.CompilerParams(collective_id=0, has_side_effects=True),
        name="exchange",
    )(occupancy, count, owner, cell, pos, vel, mpos, mvel)


def forces(halo, speeds):
    sx, sy, sz = dims = speeds.shape[1:4]
    hx, hz, slots, pairs = sx + 2, sz + 2, speeds.shape[4], sy // 2
    out = jax.ShapeDtypeStruct(speeds.shape, f32)
    vmem = pl.BlockSpec(memory_space=pltpu.VMEM)
    return pl.pallas_call(
        functools.partial(force_kernel, dims, 4 if sz % 4 == 0 else 1),
        out_shape=(out, out),
        in_specs=[vmem] * 2,
        out_specs=(vmem, vmem),
        scratch_shapes=[
            pltpu.VMEM((hx, sy, hz, slots, 48), bf16),
            pltpu.VMEM((hx, pairs, hz, slots, 96), bf16),
            pltpu.VMEM((sx, pairs, sz, 3, 48, 2 * slots), bf16),
            pltpu.VMEM((sx, pairs, sz, 3, 96, 2 * slots), bf16),
            pltpu.VMEM((hx, sy, hz, 16, 2 * slots), bf16),
            pltpu.VMEM((hx, pairs, hz, 32, 2 * slots), bf16),
            pltpu.VMEM((sx, pairs, 2, sz, 16, slots), f32),
        ],
        compiler_params=pltpu.CompilerParams(vmem_limit_bytes=32 * 1024 * 1024),
        name="forces",
    )(halo, speeds)


def per_device(
    positions, velocities, occupancy, mover_pos, mover_vel, mover_count, mover_owner, mover_cell
):
    slots, leaving = positions.shape[4], mover_pos.shape[1]
    halo, speeds = exchange(
        occupancy,
        mover_count.reshape(leaving),
        mover_owner.reshape(leaving),
        mover_cell.reshape(leaving),
        positions,
        velocities,
        mover_pos.reshape(3, leaving, 1, slots),
        mover_vel.reshape(3, leaving, 1, slots),
    )
    return forces(halo, speeds)


def solution(mesh):
    cells = P(None, "gx", "gy", "gz", None)
    labels = P("gx", "gy", "gz")
    return jax.shard_map(
        per_device,
        mesh=mesh,
        in_specs=(cells, cells, labels, cells, cells, labels, labels, labels),
        out_specs=(cells, cells),
        check_vma=False,
    )
```

profile of v0, /device:TPU:0, one launch (start us, length us, event | category | flops | bytes accessed | tf_op | source)
XLA Modules:
  0.0 25.6 jit_solution(14109662676810382372)
XLA Ops:
  0.6 14.2 %exchange.1 = (f32[3,4,10,8,128]{4,3,2,1,0:T(8,128)S(1)}, f32[3,1,2,8,128]{4,3,2,1,0:T(8,128)S(1)}) custom-call(s32[1,2,8]{2,1,0:T(2,128)} %occ_s.1, s32[3]{0:T(128)} %bitcast.7, s32[3]{0:T(128)} %bitcast.8, s32[3]{0:T(128)} %bitcast.9, f32[3,1,2,8,128]{4,3,2,1,0:T(8,128)} %pos_ref.1, f32[3,1,2,8,128]{4,3,2,1,0:T(8,128)} %vel_ref.1, ...), custom_call_target="tpu_custom_call" | custom-call | tf_op jit(solution)/shard_map/exchange/pallas_call | solution.py:336
  14.8 10.8 %forces.1 = (f32[3,1,2,8,128]{4,3,2,1,0:T(8,128)}, f32[3,1,2,8,128]{4,3,2,1,0:T(8,128)}) custom-call(f32[3,4,10,8,128]{4,3,2,1,0:T(8,128)S(1)} %get-tuple-element.4.halo_ref, f32[3,1,2,8,128]{4,3,2,1,0:T(8,128)S(1)} %get-tuple-element.5.vel_ref), custom_call_target="tpu_custom_call" | custom-call | tf_op jit(solution)/shard_map/forces/pallas_call | solution.py:359
where the time goes:
time: 25.8 us; the launch traced here: 25.6 us
  Pallas kernels  24.9 us (97%)
  between operations  0.64 us (2%)
    pallas_call x1, Pallas kernels, exchange(): pl.pallas_call(functools.partial(exchange_kernel, axes, dims, leaving), o...  14.2 us
    pallas_call x1, Pallas kernels, forces(): pl.pallas_call(functools.partial(force_kernel, dims, 4 if sz % 4 == 0 els...  10.8 us

commit v1 on v0

v1 whole, which is shorter than its diff:
```python
import functools

import jax
import jax.numpy as jnp
from jax import lax
from jax.experimental import pallas as pl
from jax.experimental.pallas import tpu as pltpu
from jax.sharding import PartitionSpec as P

eps_soft = 0.05
kick_step = 0.02
drift_step = 0.1
far_away = 1000.0

f32, bf16 = jnp.float32, jnp.bfloat16


def offsets(count):
    return sorted({0, 1 % count, count - 1})


def halo_steps():
    steps = [
        (dx, dy, dz)
        for dx in (-1, 0, 1)
        for dy in (-1, 0, 1)
        for dz in (-1, 0, 1)
        if (dx, dy, dz) != (0, 0, 0)
    ]
    return sorted(steps, key=lambda step: -sum(abs(d) for d in step))


def row_index(shape):
    return lax.broadcasted_iota(jnp.int32, shape, len(shape) - 2)


def split(value):
    high = value.astype(bf16).astype(f32)
    rest = value - high
    middle = rest.astype(bf16).astype(f32)
    return high, middle, rest - middle


def stack(high, middle, low):
    return jnp.concatenate([high, high, high, middle, middle, low], -2).astype(bf16)


def centre(dims, x, y):
    return x - 1 - 0.5 * dims[0], y - 1 - 0.5 * dims[1]


def pair_kernel(
    axes, dims, leaving, unroll, occ_h, count_h, owner_h, cell_h, pos_h, vel_h, mpos_h, mvel_h,
    halo_ref, velm_ref, total, occ_s, count_s, owner_s, cell_s, pos_ref, vel_ref, mpos_ref,
    mvel_ref, line, mov, left, left2, right, right2, src, src2, send, recv, msend, mrecv, fetch, known
):
    nx, ny, nz = axes
    sx, sy, sz = dims
    hx, hy, hz = (size + 2 for size in dims)
    slots = pos_ref.shape[-1]
    fetches = [
        pltpu.make_async_copy(there, here, fetch.at[i])
        for i, (there, here) in enumerate([
            (mpos_h, mpos_ref), (mvel_h, mvel_ref), (count_h, count_s), (owner_h, owner_s),
            (cell_h, cell_s), (occ_h, occ_s), (pos_h, pos_ref), (vel_h, vel_ref),
        ])
    ]
    for copy in fetches:
        copy.start()
    me = [lax.axis_index(name) for name in ("gx", "gy", "gz")]

    def device(step):
        return tuple(lax.rem(m + s, n) for m, s, n in zip(me, step, axes))

    def along_line(body, start):
        if nx <= 4:
            for ox in range(start, nx):
                body(ox)
        else:
            lax.fori_loop(start, nx, lambda ox, carry: (body(ox), carry)[1], 0)

    def halo_copy(step):
        source, target = [], []
        for d, size in zip(step, dims):
            if d == 0:
                source.append(pl.ds(1, size))
                target.append(pl.ds(1, size))
            elif d == 1:
                source.append(pl.ds(size, 1))
                target.append(pl.ds(0, 1))
            else:
                source.append(pl.ds(1, 1))
                target.append(pl.ds(size + 1, 1))
        number = (step[0] + 1) * 9 + (step[1] + 1) * 3 + step[2] + 1
        return pltpu.make_async_remote_copy(
            src_ref=halo_ref.at[(*source, pl.ds(0, 3))],
            dst_ref=halo_ref.at[(*target, pl.ds(0, 3))],
            send_sem=send.at[number],
            recv_sem=recv.at[number],
            device_id=device([d % n for d, n in zip(step, axes)]),
            device_id_type=pl.DeviceIdType.MESH,
        )

    def mover_copy(ox, part):
        rows = pl.ds(4 * part, 4)
        return pltpu.make_async_remote_copy(
            src_ref=mov.at[:, rows],
            dst_ref=line.at[pl.ds(me[0] * leaving, leaving), rows],
            send_sem=msend.at[part, ox],
            recv_sem=mrecv.at[part, ox],
            device_id=device((ox, 0, 0)),
            device_id_type=pl.DeviceIdType.MESH,
        )

    tile = row_index((8, slots))

    def sources(x, y, z0, z1):
        ox, oy = centre(dims, x, y)
        shift = jnp.where(tile == 0, ox, jnp.where(tile == 1, oy, -0.5)).astype(f32)
        out = {}
        for z in range(z0, z1):
            extra = jnp.where(tile == 6, 1.0, jnp.where(tile == 7, float(z - 1 - sz // 2), 0.0))
            at = jnp.where(tile < 3, halo_ref[x, y, z] + shift, 0.0)
            high, middle, low = split(at + pltpu.roll(at * at, 3, 0) + extra.astype(f32))
            both = jnp.concatenate([high, middle], 0).astype(bf16)
            out[z] = stack(high, middle, low), jnp.concatenate([both, both], 1)
        return out

    def shared_columns(x, z0, z1):
        for y in range(1, sy + 1):
            for z, (keys, twice) in sources(x, y, z0, z1).items():
                left[x, y - 1, z] = keys.T
                src[x, y - 1, z] = twice

    def split_columns(x):
        for pair in range(sy // 2):
            low, up = sources(x, 2 * pair, 0, hz), sources(x, 2 * pair + 3, 0, hz)
            for z in range(hz):
                left2[x, pair, z] = jnp.concatenate([low[z][0], up[z][0]], 0).T
                src2[x, pair, z] = jnp.concatenate([low[z][1], up[z][1]], 0)

    def targets(x, pair, z):
        tiles = []
        for y in (2 * pair, 2 * pair + 1):
            ox, oy = centre(dims, x + 1, y + 1)
            shift = jnp.where(tile == 0, ox, jnp.where(tile == 1, oy, -0.5)).astype(f32)
            at = halo_ref[x + 1, y + 1, z + 1]
            tiles.append(jnp.where(at < 0.5 * far_away, at, 0.5) + shift)
        zero = jnp.zeros((48, slots), bf16)
        for e in (-1, 0, 1):
            keys = []
            for at in tiles:
                at = jnp.where(tile < 3, at - jnp.where(tile == 2, float(e), 0.0).astype(f32), 0.0)
                norm = jnp.sum(at * at, axis=0, keepdims=True) + eps_soft
                key = jnp.where(tile < 3, -2.0 * at, jnp.where(tile < 6, 1.0, norm))
                key = jnp.where(tile < 7, key, 0.0)
                high, middle, low = split(key)
                keys.append(
                    jnp.concatenate([high, middle, low, high, middle, high], 0).astype(bf16)
                )
            right[x, pair, z, e + 1] = jnp.concatenate(keys, 1)
            right2[x, pair, z, e + 1] = jnp.concatenate(
                [jnp.concatenate([keys[0], zero], 1), jnp.concatenate([zero, keys[1]], 1)], 0
            )

    def weights(t):
        y = lax.rsqrt(t)
        a = jnp.maximum((1.0 + eps_soft) - t, 0.0) * y
        w = a * a * y
        high = w.astype(bf16)
        return jnp.concatenate([high, (w - high.astype(f32)).astype(bf16)], 0)

    def accumulate(steps, sums):
        lag = 2

        def distances(n):
            return jnp.dot(steps[n][0][...], steps[n][1][...], preferred_element_type=f32)

        queue, ready = [distances(0)], []
        for n in range(len(steps) + lag):
            if n < len(steps):
                if n + 1 < len(steps):
                    queue.append(distances(n + 1))
                ready.append(weights(queue.pop(0)))
            if n >= lag:
                step = steps[n - lag]
                sums[step[3]] = sums[step[3]] + jnp.dot(
                    step[2][...], ready.pop(0), preferred_element_type=f32
                )
        return sums

    def steps_of(columns, shared, x, pair, z, slot):
        steps = []
        for e in range(3):
            for dx in columns:
                if shared:
                    for y in (2 * pair, 2 * pair + 1):
                        steps.append((
                            left.at[dx, y, z + e], right.at[x, pair, z, e], src.at[dx, y, z + e], slot
                        ))
                else:
                    steps.append((
                        left2.at[dx, pair, z + e], right2.at[x, pair, z, e],
                        src2.at[dx, pair, z + e], slot,
                    ))
        return steps

    def phase(columns, shared, first):
        for x in range(sx):
            near_x = [dx for dx in columns if x <= dx <= x + 2]
            for pair in range(sy // 2):

                def body(i, carry, x=x, pair=pair, near_x=near_x):
                    steps = []
                    for u in range(unroll):
                        steps += steps_of(near_x, shared, x, pair, i * unroll + u, u)
                    zero = jnp.zeros((16 if shared else 32, 2 * slots), f32)
                    sums = accumulate(steps, [zero] * unroll)
                    for u in range(unroll):
                        z = i * unroll + u
                        for half in range(2):
                            rows = slice(0, 16) if shared else slice(16 * half, 16 * half + 16)
                            part = sums[u][rows, half * slots : (half + 1) * slots]
                            if not first:
                                part = part + total[x, pair, half, z]
                            total[x, pair, half, z] = part
                    return carry

                lax.fori_loop(0, sz // unroll, body, 0)

    def arrive(which):
        for step in halo_steps():
            if which(*step):
                halo_copy(step).wait_recv()

    barrier = pltpu.get_barrier_semaphore()
    ys, zs = offsets(ny)[1:], offsets(nz)[1:]

    def greet(sem, step):
        pl.semaphore_signal(
            sem, inc=1, device_id=device(step), device_id_type=pl.DeviceIdType.MESH
        )

    for oz in zs:
        greet(barrier, (0, 0, oz))
    odd = me[1] % 2
    along_line(lambda ox: greet(barrier, (ox, 0, 0)), 1)

    for copy in fetches[:5]:
        copy.wait()
    lane = lax.broadcasted_iota(jnp.int32, (1, slots), 1)
    base = me[0] * (sx * sy * sz)
    for b in range(leaving):
        live = lane < count_s[b]
        rows = [jnp.where(live, mpos_ref[k, b], far_away) for k in range(3)]
        label = owner_s[b] * (sx * sy * sz) + cell_s[b]
        rows += [jnp.full((1, slots), label, jnp.int32).astype(f32)]
        rows += [mvel_ref[k, b] for k in range(3)]
        for k, row in enumerate(rows):
            mov[b, k : k + 1, :] = row
            line[me[0] * leaving + b, k : k + 1, :] = row

    pl.semaphore_wait(barrier, nx - 1 + len(zs) + odd * len(ys))
    along_line(lambda ox: mover_copy(ox, 0).start(), 1)

    @pl.when(odd == 0)
    def _():
        for oy in ys:
            greet(barrier, (0, oy, 0))

    @pl.when(odd == 1)
    def _():
        for i, oy in enumerate(ys):
            greet(known.at[i], (0, oy, 0))

    for i, oz in enumerate(zs):
        greet(known.at[2 + i], (0, 0, oz))

    for copy in fetches[5:]:
        copy.wait()
    sub = row_index((sz, slots))
    lanes = lax.broadcasted_iota(jnp.int32, (sz, slots), 1)
    planes, where = [], []
    for x in range(sx):
        for y in range(sy):
            counts = jnp.zeros((sz, slots), jnp.int32)
            for z in range(sz):
                counts = jnp.where(sub == z, occ_s[x, y, z], counts)
            live = lanes < counts
            planes.append(
                [jnp.where(live, pos_ref[k, x, y], far_away) for k in range(3)]
            )
            where.append((sub + (base + (x * sy + y) * sz)).astype(f32))
    along_line(lambda ox: mover_copy(ox, 0).wait(), 1)

    def merge(first):
        def one(b, planes):
            label = line[b, pl.ds(3, 1), :]
            rows = [line[b, pl.ds(first + k, 1), :] for k in range(3)]
            return [
                [jnp.where(here == label, row, old) for row, old in zip(rows, plane)]
                for plane, here in zip(planes, where)
            ]

        return one

    def merged(first, planes):
        if nx <= 4:
            for b in range(nx * leaving):
                planes = merge(first)(b, planes)
            return planes
        return lax.fori_loop(0, nx * leaving, merge(first), planes)

    planes = merged(0, planes)

    flat = halo_ref.reshape((sx + 2) * (sy + 2) * (sz + 2) * 8, slots)
    for x in range(sx):
        for y in range(sy):
            first = (((x + 1) * (sy + 2) + y + 1) * (sz + 2) + 1) * 8
            for k in range(3):
                flat[pl.ds(first + k, sz, stride=8), :] = planes[x * sy + y][k]
    assert ny % 2 == 0

    def send_where(which):
        for step in halo_steps():
            if which(*step):
                halo_copy(step).start()

    send_where(lambda dx, dy, dz: abs(dx) + abs(dy) + abs(dz) == 1 and dy == 0)
    for i in range(len(zs)):
        pl.semaphore_wait(known.at[2 + i], 1)
    send_where(lambda dx, dy, dz: dx != 0 and dy == 0 and dz != 0)
    along_line(lambda ox: mover_copy(ox, 1).start(), 1)

    @pl.when(odd == 0)
    def _():
        for i in range(len(ys)):
            pl.semaphore_wait(known.at[i], 1)

    for i, oz in enumerate(zs):
        greet(known.at[4 + i], (0, 0, oz))
    send_where(lambda dx, dy, dz: dx != 0 and dy != 0 and dz == 0)
    send_where(lambda dx, dy, dz: dx == 0 and dy != 0)

    inner = range(1, sx + 1)
    for x in range(sx):
        for pair in range(sy // 2):
            for z in range(sz):
                targets(x, pair, z)
    for x in inner:
        shared_columns(x, 1, sz + 1)
    arrive(lambda dx, dy, dz: dx == 0 and dy == 0)
    for x in inner:
        shared_columns(x, 0, 1)
        shared_columns(x, sz + 1, sz + 2)
    phase(inner, True, True)
    for i in range(len(zs)):
        pl.semaphore_wait(known.at[4 + i], 1)
    send_where(lambda dx, dy, dz: dx != 0 and dy != 0 and dz != 0)
    arrive(lambda dx, dy, dz: dx != 0 and dy == 0)
    outer = (0, sx + 1)
    for x in outer:
        shared_columns(x, 0, hz)
    phase(outer, True, False)
    arrive(lambda dx, dy, dz: dy != 0)
    for x in range(hx):
        split_columns(x)
    phase(range(hx), False, False)
    along_line(lambda ox: mover_copy(ox, 1).wait(), 1)
    speeds = merged(4, [[vel_ref[k, x, y] for k in range(3)] for x in range(sx) for y in range(sy)])
    for x in range(sx):
        for y in range(sy):
            for k in range(3):
                velm_ref[k, x, y] = speeds[x * sy + y][k]
    for step in halo_steps():
        halo_copy(step).wait_send()


def kick_kernel(dims, halo_ref, vel_ref, total, npos_ref, nvel_ref):
    sx, sy, sz = dims
    hx, hy, hz = (size + 2 for size in dims)
    slots = halo_ref.shape[-1]
    flat = halo_ref.reshape(hx * hy * hz * 8, slots)
    for x in range(sx):
        for y in range(sy):
            sums = total.at[x, y // 2, y % 2].reshape(sz * 16, slots)

            def row(r, sums=sums):
                return sums[pl.ds(r, sz, stride=16), :]

            first = (((x + 1) * hy + y + 1) * hz + 1) * 8
            ox, oy = centre(dims, x + 1, y + 1)
            zat = (row_index((sz, slots)) - sz // 2).astype(f32)
            live = None
            for k, shift in enumerate((ox, oy, -0.5)):
                raw = flat[pl.ds(first + k, sz, stride=8), :]
                if k == 0:
                    live = raw < 0.5 * far_away
                high, middle, low = split(raw + shift)
                at, sum_s = high + middle, row(k) + row(8 + k)
                if k == 2:
                    at, sum_s = at + zat, sum_s + row(7)
                force = sum_s - at * row(6)
                vel = jnp.where(live, vel_ref[k, x, y] + kick_step * force, 0.0)
                nvel_ref[k, x, y] = vel
                npos_ref[k, x, y] = jnp.where(live, raw + drift_step * vel, 0.0)


def pair_sums(occupancy, count, owner, cell, pos, vel, mpos, mvel):
    axes = tuple(lax.axis_size(name) for name in ("gx", "gy", "gz"))
    sx, sy, sz = dims = pos.shape[1:4]
    leaving, slots = mpos.shape[1], mpos.shape[3]
    hx, hy, hz = padded = tuple(size + 2 for size in dims)
    pairs, wide = sy // 2, 2 * slots
    unroll = 4 if sz % 4 == 0 else 1
    vmem = pl.BlockSpec(memory_space=pltpu.VMEM)
    ints = (occupancy, count, owner, cell)
    return pl.pallas_call(
        functools.partial(pair_kernel, axes, dims, leaving, unroll),
        out_shape=(
            pltpu.VMEM((*padded, 8, slots), f32),
            pltpu.VMEM(vel.shape, f32),
            pltpu.VMEM((sx, pairs, 2, sz, 16, slots), f32),
        ),
        in_specs=[pl.BlockSpec(memory_space=pl.ANY)] * 8,
        out_specs=(vmem, vmem, vmem),
        scratch_shapes=[
            *[pltpu.SMEM(value.shape, jnp.int32) for value in ints],
            *[pltpu.VMEM(value.shape, f32) for value in (pos, vel, mpos, mvel)],
            pltpu.VMEM((axes[0] * leaving, 8, slots), f32),
            pltpu.VMEM((leaving, 8, slots), f32),
            pltpu.VMEM((hx, sy, hz, slots, 48), bf16),
            pltpu.VMEM((hx, pairs, hz, slots, 96), bf16),
            pltpu.VMEM((sx, pairs, sz, 3, 48, wide), bf16),
            pltpu.VMEM((sx, pairs, sz, 3, 96, wide), bf16),
            pltpu.VMEM((hx, sy, hz, 16, wide), bf16),
            pltpu.VMEM((hx, pairs, hz, 32, wide), bf16),
            pltpu.SemaphoreType.DMA((27,)),
            pltpu.SemaphoreType.DMA((27,)),
            pltpu.SemaphoreType.DMA((2, axes[0])),
            pltpu.SemaphoreType.DMA((2, axes[0])),
            pltpu.SemaphoreType.DMA((8,)),
            pltpu.SemaphoreType.REGULAR((6,)),
        ],
        compiler_params=pltpu.CompilerParams(collective_id=0, has_side_effects=True),
        name="pairs",
    )(*ints, pos, vel, mpos, mvel)


def kick(halo, speeds, sums):
    out = jax.ShapeDtypeStruct(speeds.shape, f32)
    vmem = pl.BlockSpec(memory_space=pltpu.VMEM)
    return pl.pallas_call(
        functools.partial(kick_kernel, speeds.shape[1:4]),
        out_shape=(out, out),
        in_specs=[vmem] * 3,
        out_specs=(vmem, vmem),
        compiler_params=pltpu.CompilerParams(vmem_limit_bytes=16 * 1024 * 1024),
        name="kick",
    )(halo, speeds, sums)


def per_device(
    positions, velocities, occupancy, mover_pos, mover_vel, mover_count, mover_owner, mover_cell
):
    slots, leaving = positions.shape[4], mover_pos.shape[1]
    halo, speeds, sums = pair_sums(
        occupancy,
        mover_count.reshape(leaving),
        mover_owner.reshape(leaving),
        mover_cell.reshape(leaving),
        positions,
        velocities,
        mover_pos.reshape(3, leaving, 1, slots),
        mover_vel.reshape(3, leaving, 1, slots),
    )
    return kick(halo, speeds, sums)


def solution(mesh):
    cells = P(None, "gx", "gy", "gz", None)
    labels = P("gx", "gy", "gz")
    return jax.shard_map(
        per_device,
        mesh=mesh,
        in_specs=(cells, cells, labels, cells, cells, labels, labels, labels),
        out_specs=(cells, cells),
        check_vma=False,
    )
```

time: 25.8 us -> 23.8 us (0.922)
  the two profiles are of different devices: /device:TPU:0 before, /device:TPU:1 now
where the time goes in v1:
time: 23.8 us; the launch traced here: 23.6 us
  Pallas kernels  23 us (97%)
  between operations  0.64 us (3%)
    pallas_call x1, Pallas kernels, pair_sums(): pl.pallas_call(functools.partial(pair_kernel, axes, dims, leaving, unroll...  22.3 us
    pallas_call x1, Pallas kernels, kick(): pl.pallas_call(functools.partial(kick_kernel, speeds.shape[1:4]), out_sha...  0.66 us

profile of v1, /device:TPU:1, one launch (start us, length us, event | category | flops | bytes accessed | tf_op | source)
XLA Modules:
  0.0 23.6 jit_solution(15779744821114201451)
XLA Ops:
  0.6 22.3 %pairs.1 = (f32[3,4,10,8,128]{4,3,2,1,0:T(8,128)S(1)}, f32[3,1,2,8,128]{4,3,2,1,0:T(8,128)S(1)}, f32[1,1,2,8,16,128]{5,4,3,2,1,0:T(8,128)S(1)}) custom-call(s32[1,2,8]{2,1,0:T(2,128)} %occ_h.1, s32[3]{0:T(128)} %bitcast.7, s32[3]{0:T(128)} %bitcast.8, s32[3]{0:T(128)} %bitcast.9, f32[3,1,2,8,128]{4,3,2,1,0:T(8,128)} %pos_h.1, f32[3,1,2,8,128]{4,3,2,1,0:T(8,128)} %vel_h.1, ...), custom_call_target="tpu_custom_call" | custom-call | tf_op jit(solution)/shard_map/pairs/pallas_call | solution.py:418
  23.0 0.7 %kick.1 = (f32[3,1,2,8,128]{4,3,2,1,0:T(8,128)}, f32[3,1,2,8,128]{4,3,2,1,0:T(8,128)}) custom-call(f32[3,4,10,8,128]{4,3,2,1,0:T(8,128)S(1)} %get-tuple-element.5.halo_ref, f32[3,1,2,8,128]{4,3,2,1,0:T(8,128)S(1)} %get-tuple-element.6.vel_ref, f32[1,1,2,8,16,128]{5,4,3,2,1,0:T(8,128)S(1)} %get-tuple-element.7.total), custom_call_target="tpu_custom_call" | custom-call | tf_op jit(solution)/shard_map/kick/pallas_call | solution.py:453

commit v2 on v1

--- a/solution.py
+++ b/solution.py
@@ -189,9 +189,9 @@
                 )
         return sums
 
-    def steps_of(columns, shared, x, pair, z, slot):
+    def steps_of(columns, shared, levels, x, pair, z, slot):
         steps = []
-        for e in range(3):
+        for e in levels:
             for dx in columns:
                 if shared:
                     for y in (2 * pair, 2 * pair + 1):
@@ -205,7 +205,7 @@
                     ))
         return steps
 
-    def phase(columns, shared, first):
+    def phase(columns, shared, levels=(0, 1, 2), first=False, unroll=unroll):
         for x in range(sx):
             near_x = [dx for dx in columns if x <= dx <= x + 2]
             for pair in range(sy // 2):
@@ -213,7 +213,7 @@
                 def body(i, carry, x=x, pair=pair, near_x=near_x):
                     steps = []
                     for u in range(unroll):
-                        steps += steps_of(near_x, shared, x, pair, i * unroll + u, u)
+                        steps += steps_of(near_x, shared, levels, x, pair, i * unroll + u, u)
                     zero = jnp.zeros((16 if shared else 32, 2 * slots), f32)
                     sums = accumulate(steps, [zero] * unroll)
                     for u in range(unroll):
@@ -244,6 +244,12 @@
     for oz in zs:
         greet(barrier, (0, 0, oz))
     odd = me[1] % 2
+
+    @pl.when(odd == 0)
+    def _():
+        for oy in ys:
+            greet(barrier, (0, oy, 0))
+
     along_line(lambda ox: greet(barrier, (ox, 0, 0)), 1)
 
     for copy in fetches[:5]:
@@ -262,11 +268,6 @@
 
     pl.semaphore_wait(barrier, nx - 1 + len(zs) + odd * len(ys))
     along_line(lambda ox: mover_copy(ox, 0).start(), 1)
-
-    @pl.when(odd == 0)
-    def _():
-        for oy in ys:
-            greet(barrier, (0, oy, 0))
 
     @pl.when(odd == 1)
     def _():
@@ -332,46 +333,53 @@
     send_where(lambda dx, dy, dz: dx != 0 and dy == 0 and dz != 0)
     along_line(lambda ox: mover_copy(ox, 1).start(), 1)
 
-    @pl.when(odd == 0)
-    def _():
-        for i in range(len(ys)):
-            pl.semaphore_wait(known.at[i], 1)
-
-    for i, oz in enumerate(zs):
-        greet(known.at[4 + i], (0, 0, oz))
-    send_where(lambda dx, dy, dz: dx != 0 and dy != 0 and dz == 0)
-    send_where(lambda dx, dy, dz: dx == 0 and dy != 0)
-
-    inner = range(1, sx + 1)
+    inner, outer = range(1, sx + 1), (0, sx + 1)
     for x in range(sx):
         for pair in range(sy // 2):
             for z in range(sz):
                 targets(x, pair, z)
     for x in inner:
         shared_columns(x, 1, sz + 1)
-    arrive(lambda dx, dy, dz: dx == 0 and dy == 0)
-    for x in inner:
-        shared_columns(x, 0, 1)
-        shared_columns(x, sz + 1, sz + 2)
-    phase(inner, True, True)
-    for i in range(len(zs)):
-        pl.semaphore_wait(known.at[4 + i], 1)
-    send_where(lambda dx, dy, dz: dx != 0 and dy != 0 and dz != 0)
-    arrive(lambda dx, dy, dz: dx != 0 and dy == 0)
-    outer = (0, sx + 1)
-    for x in outer:
-        shared_columns(x, 0, hz)
-    phase(outer, True, False)
-    arrive(lambda dx, dy, dz: dy != 0)
-    for x in range(hx):
-        split_columns(x)
-    phase(range(hx), False, False)
+    @pl.when(odd == 0)
+    def _():
+        for i, oy in enumerate(ys):
+            pl.semaphore_wait(known.at[i], 1)
+        for i, oy in enumerate(ys):
+            greet(known.at[i], (0, oy, 0))
+
+    phase(inner, True, (1,), True, sz)
+
+    @pl.when(odd == 1)
+    def _():
+        for i in range(len(ys)):
+            pl.semaphore_wait(known.at[i], 1)
+
+    for i, oz in enumerate(zs):
+        greet(known.at[4 + i], (0, 0, oz))
+    send_where(lambda dx, dy, dz: dx != 0 and dy != 0 and dz == 0)
+    send_where(lambda dx, dy, dz: dx == 0 and dy != 0)
     along_line(lambda ox: mover_copy(ox, 1).wait(), 1)
     speeds = merged(4, [[vel_ref[k, x, y] for k in range(3)] for x in range(sx) for y in range(sy)])
     for x in range(sx):
         for y in range(sy):
             for k in range(3):
                 velm_ref[k, x, y] = speeds[x * sy + y][k]
+    arrive(lambda dx, dy, dz: dx == 0 and dy == 0)
+    for x in inner:
+        shared_columns(x, 0, 1)
+        shared_columns(x, sz + 1, sz + 2)
+    for i in range(len(zs)):
+        pl.semaphore_wait(known.at[4 + i], 1)
+    send_where(lambda dx, dy, dz: dx != 0 and dy != 0 and dz != 0)
+    phase(inner, True, (0, 2), False, sz)
+    arrive(lambda dx, dy, dz: dx != 0 and dy == 0)
+    for x in outer:
+        shared_columns(x, 0, hz)
+    phase(outer, True)
+    arrive(lambda dx, dy, dz: dy != 0)
+    for x in range(hx):
+        split_columns(x)
+    phase(range(hx), False)
     for step in halo_steps():
         halo_copy(step).wait_send()
 

time: 23.8 us -> 22.7 us (0.954)
  the two profiles are of different devices: /device:TPU:1 before, /device:TPU:0 now
where the time goes in v2:
time: 22.7 us; the launch traced here: 22.5 us
  Pallas kernels  21.8 us (96%)
  between operations  0.64 us (3%)
    pallas_call x1, Pallas kernels, pair_sums(): pl.pallas_call(functools.partial(pair_kernel, axes, dims, leaving, unroll...  21.2 us
    pallas_call x1, Pallas kernels, kick(): pl.pallas_call(functools.partial(kick_kernel, speeds.shape[1:4]), out_sha...  0.66 us

profile of v2, /device:TPU:0, one launch (start us, length us, event | category | flops | bytes accessed | tf_op | source)
XLA Modules:
  0.0 22.5 jit_solution(8200026184067452446)
XLA Ops:
  0.6 21.2 %pairs.1 = (f32[3,4,10,8,128]{4,3,2,1,0:T(8,128)S(1)}, f32[3,1,2,8,128]{4,3,2,1,0:T(8,128)S(1)}, f32[1,1,2,8,16,128]{5,4,3,2,1,0:T(8,128)S(1)}) custom-call(s32[1,2,8]{2,1,0:T(2,128)} %occ_h.1, s32[3]{0:T(128)} %bitcast.7, s32[3]{0:T(128)} %bitcast.8, s32[3]{0:T(128)} %bitcast.9, f32[3,1,2,8,128]{4,3,2,1,0:T(8,128)} %pos_h.1, f32[3,1,2,8,128]{4,3,2,1,0:T(8,128)} %vel_h.1, ...), custom_call_target="tpu_custom_call" | custom-call | tf_op jit(solution)/shard_map/pairs/pallas_call | solution.py:426
  21.8 0.7 %kick.1 = (f32[3,1,2,8,128]{4,3,2,1,0:T(8,128)}, f32[3,1,2,8,128]{4,3,2,1,0:T(8,128)}) custom-call(f32[3,4,10,8,128]{4,3,2,1,0:T(8,128)S(1)} %get-tuple-element.5.halo_ref, f32[3,1,2,8,128]{4,3,2,1,0:T(8,128)S(1)} %get-tuple-element.6.vel_ref, f32[1,1,2,8,16,128]{5,4,3,2,1,0:T(8,128)S(1)} %get-tuple-element.7.total), custom_call_target="tpu_custom_call" | custom-call | tf_op jit(solution)/shard_map/kick/pallas_call | solution.py:461
